TPU v7x, 32 devices: a whole 2x2x4 slice. The times are simulated.
32 devices in a mesh: row: 8 (over z, y), col: 4 (over x, core).
Axes of the slice: x: 2, y: 2, z: 4, core: 2. Of those that a mesh axis runs over, the one named last changes fastest.
Arguments:
- features: float32 [32, 3072], P(None, ('row', 'col')), may hold values from -6 to 6
- block: float32 [16, 3072], P(None, ('row', 'col')), may hold values from -6 to 6
Outputs:
- applied: float32 [16, 3072], P(None, ('row', 'col'))
All inputs are finite; a program needn't handle non-finite values.
Results may differ from a plain program's by a relative error of at most 0.006.
Values may be sent and summed in bfloat16 or wider, within the bound.
A program may use at most 64 MiB of HBM per device.

v0:
```python
import math
import jax
import jax.numpy as jnp
from jax import lax
from jax.sharding import PartitionSpec as P


def kernel_rows(row_feat, row_sq, col_feat, col_sq, scale, start, count):
    part = lax.dynamic_slice_in_dim(row_feat, start, count, 1)
    sq_part = lax.dynamic_slice_in_dim(row_sq, start, count, 0)
    inner = jnp.einsum("fi,fj->ij", part, col_feat, precision=lax.Precision.HIGHEST)
    dist = sq_part[:, None] + col_sq[None, :] - 2.0 * inner
    return jnp.exp(-dist / scale).astype(jnp.bfloat16)


def combine(partial_value, owned):
    whole = lax.psum(partial_value, "col")
    return lax.dynamic_slice_in_dim(whole, lax.axis_index("col") * owned, owned, 1)


def full_plan(features, block, row_feat, scale):
    owned = features.shape[1]
    col_feat = lax.all_gather(features, "row", axis=1, tiled=True)
    row_sq = jnp.sum(row_feat * row_feat, axis=0)
    col_sq = jnp.sum(col_feat * col_feat, axis=0)
    rows = row_feat.shape[1]
    step = math.gcd(512, rows)
    count_blocks = rows // step
    starts = jnp.arange(count_blocks, dtype=jnp.int32) * step
    indexes = jnp.arange(count_blocks, dtype=jnp.int32)

    def fetch(index):
        return kernel_rows(row_feat, row_sq, col_feat, col_sq, scale, starts[index], step)

    def first_pass(index):
        tile = fetch(index)
        return (jnp.sum(tile, axis=1, dtype=jnp.float32), jnp.sum(tile, axis=0, dtype=jnp.float32))

    row_parts, col_parts = lax.map(first_pass, indexes)
    q_own = combine(row_parts.reshape(1, rows), owned)
    inv_own = 1.0 / q_own
    col_total = lax.psum(jnp.sum(col_parts, axis=0)[None, :], "row")
    inv_col = 1.0 / col_total

    def second_pass(index):
        return jnp.sum(fetch(index).astype(jnp.float32) * inv_col, axis=1)

    second = combine(lax.map(second_pass, indexes).reshape(1, rows), owned)
    dens = second * inv_own
    factor = inv_own * lax.rsqrt(dens)
    weighted = (block * factor).astype(jnp.bfloat16)
    weighted_col = lax.all_gather(weighted, "row", axis=1, tiled=True)

    def third_pass(index):
        return jnp.einsum(
            "kj,ij->ki", weighted_col, fetch(index), preferred_element_type=jnp.float32
        )

    products = lax.map(third_pass, indexes)
    partial_value = jnp.moveaxis(products, 0, 1).reshape(block.shape[0], rows)
    return combine(partial_value, owned) * factor


def per_device(features, block):
    n_row = lax.axis_size("row")
    n_col = lax.axis_size("col")
    width, owned = features.shape
    frames = owned * n_row * n_col
    scale = 4.0 / (float(frames) ** (2.0 / width) - 1.0)
    row_feat = lax.all_gather(features, "col", axis=1, tiled=True)
    return full_plan(features, block, row_feat, scale)


def solution(mesh):
    placed = (P(None, ("row", "col")), P(None, ("row", "col")))
    return jax.shard_map(
        per_device, mesh=mesh, in_specs=placed, out_specs=P(None, ("row", "col")), check_vma=False
    )
```

profile of v0, /device:TPU:0, one launch (start us, length us, event | category | flops | bytes accessed | tf_op | source)
XLA Modules:
  0.0 166.0 jit_solution(17195008290931523014)
XLA Ops:
  0.0 32.5 %all-gather.1 = f32[8,96,32]{1,2,0:T(8,128)S(1)} all-gather(f32[1,96,32]{1,2,0:T(8,128)} %bitcast.84), channel_id=1, replica_groups=mesh['row'=8,'col'=4] {'row'}, dimensions={0}, use_global_device_ids=true | all-gather | bytes 110592 | tf_op jit(solution)/shard_map/all_gather | solution.py:23
  32.5 0.1 copy.13
  32.6 0.1 reshape.21
  32.8 0.7 copy-done
  33.4 5.2 %all-gather = f32[4,96,32]{1,2,0:T(8,128)S(1)} all-gather(f32[1,96,32]{1,2,0:T(8,128)S(1)} %bitcast.85), channel_id=1, replica_groups=mesh['row'=8,'col'=4] {'col'}, dimensions={0}, use_global_device_ids=true | all-gather | bytes 61440 | tf_op jit(solution)/shard_map/all_gather | solution.py:70
  38.7 0.1 reshape.19
  38.9 19.3 %while.32 = (s32[]{:T(128)}, f32[3,128]{1,0:T(4,128)S(1)}, f32[3,768]{1,0:T(4,128)S(1)}, s32[3]{0:T(128)S(1)}, s32[3]{0:T(128)S(1)}, /*index=5*/f32[384]{0:T(512...) while((s32[]{:T(128)}, f32[3,128]{1,0:T(4,128)S(1)}, ...), condition=%wide.region_5.6_spmd, body=%wide.region_2.5_spmd.sunk | while | flops 38632584 | bytes 137449 | solution.py:39
  38.9 0.7 dynamic_slice.87
  41.6 0.7 dynamic_slice.88
  44.4 0.1 dynamic_slice.89
  44.5 0.7 fusion.51
  45.3 0.7 dynamic_slice.87
  48.1 0.7 dynamic_slice.88
  50.9 0.7 fusion.51
  51.8 0.7 dynamic_slice.87
  54.5 0.7 dynamic_slice.88
  57.3 0.7 fusion.51
  58.2 21.4 %psum.29 = f32[1,768]{1,0:T(1,128)S(1)} all-reduce(f32[1,768]{1,0:T(1,128)S(1)} %broadcast_in_dim.32), channel_id=1, replica_groups=mesh['row'=8,'col'=4] {'row'}, use_global_device_ids=true, to_apply=%region_8.9 | all-reduce | flops 768 | bytes 6144 | tf_op jit(solution)/shard_map/psum | solution.py:42
  79.6 19.1 %while.33 = (s32[]{:T(128)}, f32[3,128]{1,0:T(4,128)S(1)}, s32[3]{0:T(128)S(1)}, s32[3]{0:T(128)S(1)}, f32[384]{0:T(512)S(1)}, /*index=5*/f32[768]{0:T(1024)S(1)...) while((s32[]{:T(128)}, f32[3,128]{1,0:T(4,128)S(1)}, ...), condition=%wide.region_11.12_spmd, body=%wide.region_9.11_spmd.sunk | while | flops 38633352 | bytes 132337 | solution.py:48
  79.6 0.7 dynamic_slice.91
  82.4 0.7 dynamic_slice.92
  85.2 0.7 fusion.54
  86.0 0.7 dynamic_slice.91
  88.7 0.7 dynamic_slice.92
  91.6 0.7 fusion.54
  92.3 0.7 dynamic_slice.91
  95.1 0.7 dynamic_slice.92
  97.9 0.7 fusion.54
  98.7 5.7 %all-reduce = (f32[1,384]{1,0:T(1,128)S(1)}, f32[1,384]{1,0:T(1,128)S(1)}) all-reduce(f32[1,384]{1,0:T(1,128)S(1)} %get-tuple-element.209, f32[1,384]{1,0:T(1,128)S(1)} %get-tuple-element.210), channel_id=1, replica_groups=mesh['row'=8,'col'=4] {'col'}, use_global_device_ids=true, to_apply=%region_12.13 | all-reduce | flops 768 | bytes 6144 | tf_op jit(solution)/shard_map/psum | solution.py:17
  104.5 0.6 copy-done.1
  105.1 30.6 %all-gather.2 = bf16[8,96,16]{1,2,0:T(8,128)(2,1)S(1)} all-gather(bf16[1,96,16]{1,2,0:T(8,128)(2,1)S(1)} %fusion.26), channel_id=1, replica_groups=mesh['row'=8,'col'=4] {'row'}, dimensions={0}, use_global_device_ids=true | all-gather | bytes 27648 | tf_op jit(solution)/shard_map/all_gather | solution.py:52
  135.7 0.1 reshape.23
  135.8 19.2 %while.34 = (s32[]{:T(128)}, f32[3,16,128]{2,1,0:T(8,128)S(1)}, s32[3]{0:T(128)S(1)}, s32[3]{0:T(128)S(1)}, f32[384]{0:T(512)S(1)}, /*index=5*/f32[768]{0:T(1024...) while((s32[]{:T(128)}, f32[3,16,128]{2,1,0:T(8,128)S(1)}, ...), condition=%wide.region_14.15_spmd, body=%wide.region_13.14_spmd.sunk | while | flops 41484296 | bytes 546533 | solution.py:59
  135.8 0.7 dynamic_slice.95
  138.6 0.7 dynamic_slice.96
  141.3 0.1 dynamic_slice.97
  141.4 0.6 fusion.59
  142.0 0.1 fusion.60
  142.2 0.7 dynamic_slice.95
  145.0 0.7 dynamic_slice.96
  147.8 0.6 fusion.59
  148.4 0.1 fusion.60
  148.6 0.7 dynamic_slice.95
  151.4 0.7 dynamic_slice.96
  154.2 0.6 fusion.59
  154.8 0.1 fusion.60
  155.0 10.3 %psum.31 = f32[16,384]{1,0:T(8,128)S(1)} all-reduce(f32[16,384]{1,0:T(8,128)S(1)} %copy_bitcast_fusion), channel_id=1, replica_groups=mesh['row'=8,'col'=4] {'col'}, use_global_device_ids=true, to_apply=%region_15.16 | all-reduce | flops 6144 | bytes 49152 | tf_op jit(solution)/shard_map/psum | solution.py:17
  165.3 0.7 dynamic-slice_multiply_fusion
  (43 shorter events, 1.3 us)
Async XLA Ops:
  32.7 0.7 copy-start
  104.4 0.7 copy-start.1
where the time goes:
time: 167 us; the launch traced here: 166 us
  blocking collectives  106 us (63%)
  loops' own time  37.5 us (22%)
  local copies, waits for them, and re-layouts  15 us (9%)
  matrix products  6.79 us (4%)
    all_gather x1, blocking collectives, full_plan(): col_feat = lax.all_gather(features, 'row', axis=1, tiled=True)  32.5 us
    all_gather x1, blocking collectives, full_plan(): weighted_col = lax.all_gather(weighted, 'row', axis=1, tiled=True)  30.6 us
    psum x1, blocking collectives, full_plan(): col_total = lax.psum(jnp.sum(col_parts, axis=0)[None, :], 'row')  21.4 us
    psum x2, blocking collectives, combine(): whole = lax.psum(partial_value, 'col')  16 us
    another operation x1, loops' own time, full_plan(): row_parts, col_parts = lax.map(first_pass, indexes)  12.5 us
    another operation x1, loops' own time, full_plan(): products = lax.map(third_pass, indexes)  12.5 us
    another operation x1, loops' own time, full_plan(): second = combine(lax.map(second_pass, indexes).reshape(1, rows), owned)  12.5 us
    dot_general x9, matrix products, kernel_rows(): jnp.einsum('fi,fj->ij', part, col_feat, precision=lax.Precision.HIGHEST)  6.41 us

commit v1 on v0

--- a/solution.py
+++ b/solution.py
@@ -20,7 +20,10 @@
 
 def full_plan(features, block, row_feat, scale):
     owned = features.shape[1]
-    col_feat = lax.all_gather(features, "row", axis=1, tiled=True)
+    peers = lax.axis_size("row")
+    blocks = jnp.stack([features for _ in range(peers)])
+    blocks = lax.all_to_all(blocks, "row", split_axis=0, concat_axis=0)
+    col_feat = jnp.concatenate(blocks, axis=1)
     row_sq = jnp.sum(row_feat * row_feat, axis=0)
     col_sq = jnp.sum(col_feat * col_feat, axis=0)
     rows = row_feat.shape[1]

time: 167 us -> 142 us (0.85)
  blocking collectives: 106 us -> 71.8 us
  starting transfers between devices: 0 us -> 7.44 us
  waiting for transfers between devices: 0 us -> 1.9 us
    all_gather x1 -> x0, blocking collectives: 32.5 us -> none  [full_plan(): col_feat = lax.all_gather(features, 'row', axis=1, tiled=True)]
    all_to_all x0 -> x1, starting transfers between devices: none -> 7.44 us  [full_plan(): blocks = lax.all_to_all(blocks, 'row', split_axis=0, concat_axis=0)]
    all_to_all x0 -> x1, waiting for transfers between devices: none -> 1.9 us  [full_plan(): blocks = lax.all_to_all(blocks, 'row', split_axis=0, concat_axis=0)]
  transfers between devices with their start and end apart: 0 -> 1, of which waited for: 0 -> 1; matrix products, arithmetic and copies ran while one was open for 0% -> 0% of each run, Pallas kernels for 0% -> 0%
where the time goes in v1:
time: 142 us; the launch traced here: 141 us
  blocking collectives  71.8 us (51%)
  loops' own time  37.5 us (26%)
  local copies, waits for them, and re-layouts  15.1 us (11%)
  starting transfers between devices  7.44 us (5%)
  matrix products  6.79 us (5%)
  waiting for transfers between devices  1.9 us (1%)
    all_gather x1, blocking collectives, full_plan(): weighted_col = lax.all_gather(weighted, 'row', axis=1, tiled=True)  30.6 us
    psum x1, blocking collectives, full_plan(): col_total = lax.psum(jnp.sum(col_parts, axis=0)[None, :], 'row')  19.9 us
    psum x2, blocking collectives, combine(): whole = lax.psum(partial_value, 'col')  16 us
    another operation x1, loops' own time, full_plan(): row_parts, col_parts = lax.map(first_pass, indexes)  12.5 us
    another operation x1, loops' own time, full_plan(): products = lax.map(third_pass, indexes)  12.5 us
    another operation x1, loops' own time, full_plan(): second = combine(lax.map(second_pass, indexes).reshape(1, rows), owned)  12.5 us
    all_to_all x1, starting transfers between devices, full_plan(): blocks = lax.all_to_all(blocks, 'row', split_axis=0, concat_axis=0)  7.44 us
    dot_general x9, matrix products, kernel_rows(): jnp.einsum('fi,fj->ij', part, col_feat, precision=lax.Precision.HIGHEST)  6.41 us
  transfers between devices with their start and end apart: 1, of which 1 were waited for; matrix products, arithmetic and copies ran while one was open for 0% of the time, Pallas kernels for 0%

profile of v1, /device:TPU:0, one launch (start us, length us, event | category | flops | bytes accessed | tf_op | source)
XLA Modules:
  0.0 141.5 jit_solution(8643121587314181985)
XLA Ops:
  0.0 1.4 stack.2
  1.4 7.4 %all-to-all-start = ((f32[8,32,96]{2,1,0:T(8,128)}), f32[8,32,96]{2,1,0:T(8,128)S(1)}, u32[]{:S(2)}, u32[]{:S(2)}) async-start(f32[8,32,96]{2,1,0:T(8,128)} %stack.2), calls=%async_computation | async-start | bytes 262144 | tf_op jit(solution)/shard_map/all_to_all | solution.py:25
  8.8 5.2 %all-gather = f32[4,96,32]{1,2,0:T(8,128)S(1)} all-gather(f32[1,96,32]{1,2,0:T(8,128)S(1)} %bitcast.82), channel_id=1, replica_groups=mesh['row'=8,'col'=4] {'col'}, dimensions={0}, use_global_device_ids=true | all-gather | bytes 61440 | tf_op jit(solution)/shard_map/all_gather | solution.py:73
  14.1 0.1 reshape.30
  14.2 1.9 %all-to-all-done = f32[8,32,96]{2,1,0:T(8,128)S(1)} async-done(((f32[8,32,96]{2,1,0:T(8,128)}), f32[8,32,96]{2,1,0:T(8,128)S(1)}, u32[]{:S(2)}, u32[]{:S(2)}) %all-to-all-start) | async-done | bytes 98336 | tf_op jit(solution)/shard_map/all_to_all | solution.py:25
  16.2 0.1 copy.11
  16.2 0.1 reshape.25
  16.4 19.3 %while.32 = (s32[]{:T(128)}, f32[3,128]{1,0:T(4,128)S(1)}, f32[3,768]{1,0:T(4,128)S(1)}, s32[3]{0:T(128)S(1)}, s32[3]{0:T(128)S(1)}, /*index=5*/f32[384]{0:T(512...) while((s32[]{:T(128)}, f32[3,128]{1,0:T(4,128)S(1)}, ...), condition=%wide.region_5.6_spmd, body=%wide.region_2.5_spmd.sunk | while | flops 38632584 | bytes 137449 | solution.py:42
  16.4 0.7 dynamic_slice.87
  19.2 0.7 dynamic_slice.88
  21.9 0.1 dynamic_slice.89
  22.0 0.7 fusion.51
  22.9 0.7 dynamic_slice.87
  25.6 0.7 dynamic_slice.88
  28.4 0.1 dynamic_slice.89
  28.4 0.7 fusion.51
  29.3 0.7 dynamic_slice.87
  32.0 0.7 dynamic_slice.88
  34.9 0.7 fusion.51
  35.8 19.9 %psum.29 = f32[1,768]{1,0:T(1,128)S(1)} all-reduce(f32[1,768]{1,0:T(1,128)S(1)} %broadcast_in_dim.32), channel_id=1, replica_groups=mesh['row'=8,'col'=4] {'row'}, use_global_device_ids=true, to_apply=%region_8.9 | all-reduce | flops 768 | bytes 6144 | tf_op jit(solution)/shard_map/psum | solution.py:45
  55.7 19.1 %while.33 = (s32[]{:T(128)}, f32[3,128]{1,0:T(4,128)S(1)}, s32[3]{0:T(128)S(1)}, s32[3]{0:T(128)S(1)}, f32[384]{0:T(512)S(1)}, /*index=5*/f32[768]{0:T(1024)S(1)...) while((s32[]{:T(128)}, f32[3,128]{1,0:T(4,128)S(1)}, ...), condition=%wide.region_11.12_spmd, body=%wide.region_9.11_spmd.sunk | while | flops 38633352 | bytes 132337 | solution.py:51
  55.7 0.7 dynamic_slice.91
  58.5 0.7 dynamic_slice.92
  61.3 0.7 fusion.54
  62.1 0.7 dynamic_slice.91
  64.8 0.7 dynamic_slice.92
  67.7 0.7 fusion.54
  68.5 0.7 dynamic_slice.91
  71.2 0.7 dynamic_slice.92
  74.0 0.7 fusion.54
  74.9 5.7 %all-reduce = (f32[1,384]{1,0:T(1,128)S(1)}, f32[1,384]{1,0:T(1,128)S(1)}) all-reduce(f32[1,384]{1,0:T(1,128)S(1)} %get-tuple-element.209, f32[1,384]{1,0:T(1,128)S(1)} %get-tuple-element.210), channel_id=1, replica_groups=mesh['row'=8,'col'=4] {'col'}, use_global_device_ids=true, to_apply=%region_12.13 | all-reduce | flops 768 | bytes 6144 | tf_op jit(solution)/shard_map/psum | solution.py:17
  80.6 30.6 %all-gather.1 = bf16[8,96,16]{1,2,0:T(8,128)(2,1)S(1)} all-gather(bf16[1,96,16]{1,2,0:T(8,128)(2,1)S(1)} %fusion.26), channel_id=1, replica_groups=mesh['row'=8,'col'=4] {'row'}, dimensions={0}, use_global_device_ids=true | all-gather | bytes 27648 | tf_op jit(solution)/shard_map/all_gather | solution.py:55
  111.2 0.1 reshape.32
  111.3 19.2 %while.34 = (s32[]{:T(128)}, f32[3,16,128]{2,1,0:T(8,128)S(1)}, s32[3]{0:T(128)S(1)}, s32[3]{0:T(128)S(1)}, f32[384]{0:T(512)S(1)}, /*index=5*/f32[768]{0:T(1024...) while((s32[]{:T(128)}, f32[3,16,128]{2,1,0:T(8,128)S(1)}, ...), condition=%wide.region_14.15_spmd, body=%wide.region_13.14_spmd.sunk | while | flops 41484296 | bytes 546533 | solution.py:62
  111.4 0.7 dynamic_slice.95
  114.1 0.7 dynamic_slice.96
  116.9 0.6 fusion.59
  117.6 0.1 fusion.60
  117.7 0.7 dynamic_slice.95
  120.5 0.7 dynamic_slice.96
  123.3 0.6 fusion.59
  124.0 0.1 fusion.60
  124.1 0.7 dynamic_slice.95
  126.9 0.7 dynamic_slice.96
  129.7 0.6 fusion.59
  130.4 0.1 fusion.60
  130.5 10.3 %psum.31 = f32[16,384]{1,0:T(8,128)S(1)} all-reduce(f32[16,384]{1,0:T(8,128)S(1)} %copy_bitcast_fusion), channel_id=1, replica_groups=mesh['row'=8,'col'=4] {'col'}, use_global_device_ids=true, to_apply=%region_15.16 | all-reduce | flops 6144 | bytes 49152 | tf_op jit(solution)/shard_map/psum | solution.py:17
  140.8 0.7 dynamic-slice_multiply_fusion
  (46 shorter events, 1.3 us)
Async XLA Ops:
  1.4 7.5 %copy-start = (f32[32,96]{1,0:T(8,128)S(1)}, f32[32,96]{1,0:T(8,128)}, u32[]{:S(2)}) copy-start(f32[32,96]{1,0:T(8,128)} %param.8) | copy-start | bytes 36868
  1.4 14.8 %all-to-all-start = ((f32[8,32,96]{2,1,0:T(8,128)}), f32[8,32,96]{2,1,0:T(8,128)S(1)}, u32[]{:S(2)}, u32[]{:S(2)}) async-start(f32[8,32,96]{2,1,0:T(8,128)} %stack.2), calls=%async_computation | async-start | bytes 262144 | tf_op jit(solution)/shard_map/all_to_all | solution.py:25
  74.8 5.8 %copy-start.1 = (f32[16,96]{1,0:T(8,128)S(1)}, f32[16,96]{1,0:T(8,128)}, u32[]{:S(2)}) copy-start(f32[16,96]{1,0:T(8,128)} %param.9) | copy-start | bytes 18436
